TPU v7x, 32 devices: a whole 2x2x4 slice. The times are simulated.
32 devices in a mesh: dom: 16 (over z, y, x), st: 2 (over core).
Axes of the slice: x: 2, y: 2, z: 4, core: 2. Of those that a mesh axis runs over, the one named last changes fastest.
Arguments:
- psi: float32 [2, 16, 8, 2, 64, 256], P(None, 'dom', None, None, None, 'st'), parts along dimension 5, may hold values from -18 to 18
- potential: float32 [16, 8, 2, 64], P('dom'), may hold values from 0 to 4
Outputs:
- propagated: float32 [2, 16, 8, 2, 64, 256], P(None, 'dom', None, None, None, 'st'), parts along dimension 5
There are 2 independent parts, one for each index of `st`. A program takes and returns all parts, laid end to end along the dimension named above; an argument that names none is the same for every part. Nothing has to cross between parts.
All inputs are finite; a program needn't handle non-finite values.
Results may differ from a plain program's by a relative error of at most 0.0003.
Values sent between devices are 32-bit elements; how exact they have to be, the bound alone decides.
A program may use at most 128 MiB of HBM per device.

v0:
```python
import functools

import jax
import jax.numpy as jnp
from jax import lax
from jax.experimental import pallas as pl
from jax.experimental.pallas import tpu as pltpu
from jax.sharding import PartitionSpec as P

ITERS = 6


epsilon = 1e-06
time_step = 0.5
taylor_terms = 32
far_weight = -1.0 / 12.0
near_weight = 4.0 / 3.0
centre_weight = -7.5


def to_grid(blocked):
    parts, nblocks, cx, by, nz, orbs = blocked.shape
    grid = blocked.transpose(0, 2, 1, 3, 4, 5)
    return grid.reshape(parts, cx, nblocks * by, nz, orbs)


def to_blocks(grid, by):
    parts, nx, ny, nz, orbs = grid.shape
    blocked = grid.reshape(parts, nx, ny // by, by, nz, orbs).transpose(0, 2, 1, 3, 4, 5)
    return blocked


def shift_walls(values, offset):
    width_y = values.shape[2]
    padded = jnp.pad(values, ((0, 0), (0, 0), (2, 2), (0, 0), (0, 0)))
    return padded[:, :, 2 - offset : 2 - offset + width_y]


def hamiltonian_whole(values_in, potential):
    total = centre_weight * values_in
    for along in (1, 3):
        total = total + near_weight * (
            jnp.roll(values_in, 1, along) + jnp.roll(values_in, -1, along)
        )
        total = total + far_weight * (
            jnp.roll(values_in, 2, along) + jnp.roll(values_in, -2, along)
        )
    total = total + near_weight * (shift_walls(values_in, 1) + shift_walls(values_in, -1))
    total = total + far_weight * (shift_walls(values_in, 2) + shift_walls(values_in, -2))
    return -0.5 * total + potential[None, :, :, :, None] * values_in


def tridiagonal(alphas, betas, vector):
    zero_row = jnp.zeros((1, vector.shape[1]), jnp.float32)
    upper = jnp.concatenate([betas * vector[1:], zero_row], axis=0)
    lower = jnp.concatenate([zero_row, betas * vector[:-1]], axis=0)
    return alphas * vector + upper + lower


def krylov_exponential(alphas, betas):
    count = alphas.shape[0]
    first = (jnp.arange(count) == 0).astype(jnp.float32)[:, None] * jnp.ones_like(alphas)
    term_real = first
    term_imag = jnp.zeros_like(alphas)
    sum_real = term_real
    sum_imag = term_imag
    for order in range(1, taylor_terms):
        applied_real = tridiagonal(alphas, betas, term_real)
        applied_imag = tridiagonal(alphas, betas, term_imag)
        term_real = time_step * applied_imag / order
        term_imag = -time_step * applied_real / order
        sum_real = sum_real + term_real
        sum_imag = sum_imag + term_imag
    return (sum_real, sum_imag)


def combine_basis(krylov_basis, alpha_list, beta_list, first_norm):
    coef_real, coef_imag = krylov_exponential(jnp.stack(alpha_list), jnp.stack(beta_list))
    out_real = jnp.zeros_like(krylov_basis[0][0])
    out_imag = jnp.zeros_like(krylov_basis[0][0])
    for index_j in range(len(krylov_basis)):
        basis_now = krylov_basis[index_j]
        out_real = out_real + coef_real[index_j] * basis_now[0] - coef_imag[index_j] * basis_now[1]
        out_imag = out_imag + coef_real[index_j] * basis_now[1] + coef_imag[index_j] * basis_now[0]
    return first_norm * jnp.stack([out_real, out_imag])


def local_lanczos(grid_psi, grid_pot):
    axes_all = (0, 1, 2, 3)
    first_norm = jnp.sqrt(jnp.sum(grid_psi * grid_psi, axis=axes_all) + epsilon)
    vector = grid_psi / first_norm
    previous = jnp.zeros_like(vector)
    beta_prev = jnp.zeros_like(first_norm)
    krylov_basis = []
    alpha_list = []
    beta_list = []
    for iteration in range(ITERS):
        applied = hamiltonian_whole(vector, grid_pot)
        alpha_now = jnp.sum(vector * applied, axis=axes_all)
        krylov_basis.append(vector)
        alpha_list.append(alpha_now)
        if iteration + 1 < ITERS:
            remainder = applied - alpha_now * vector - beta_prev * previous
            beta_now = jnp.sqrt(jnp.sum(remainder * remainder, axis=axes_all) + epsilon)
            previous = vector
            vector = remainder / beta_now
            beta_prev = beta_now
            beta_list.append(beta_now)
    return combine_basis(krylov_basis, alpha_list, beta_list, first_norm)


def on_device(psi, potential):
    by = psi.shape[3]
    moved = lax.all_to_all(psi, "dom", split_axis=5, concat_axis=1, tiled=True)
    whole_pot = lax.all_gather(potential, "dom", axis=0, tiled=True)
    grid_pot = to_grid(whole_pot[None, :, :, :, :, None])[0, :, :, :, 0]
    result = to_blocks(local_lanczos(to_grid(moved), grid_pot), by)
    return lax.all_to_all(result, "dom", split_axis=1, concat_axis=5, tiled=True)


SUB = 8
LANES = 128
HALF = SUB // 2
CHUNKS = 2
GROUP = 4
UNROLL_A = 4
UNROLL_B = 8


def swap_parts(x):
    return pltpu.roll(x, HALF, 0)


def total_of(acc):
    summed = jnp.broadcast_to(jnp.sum(acc, axis=1, keepdims=True), (SUB, LANES))
    return summed + swap_parts(summed)


def krylov_weights(alphas, betas):
    count = len(alphas)
    one = jnp.ones((SUB, LANES), jnp.float32)
    term = [one] + [None] * (count - 1)
    real = [one] + [None] * (count - 1)
    imag = [None] * count
    for order in range(1, taylor_terms):
        fresh = []
        for i in range(count):
            pieces = []
            if term[i] is not None:
                pieces.append(alphas[i] * term[i])
            if i + 1 < count and term[i + 1] is not None:
                pieces.append(betas[i] * term[i + 1])
            if i > 0 and term[i - 1] is not None:
                pieces.append(betas[i - 1] * term[i - 1])
            fresh.append(sum(pieces[1:], pieces[0]) * (time_step / order) if pieces else None)
        term = fresh
        into = imag if order % 2 else real
        minus = order % 4 in (1, 2)
        for i in range(count):
            if term[i] is not None:
                if into[i] is None:
                    into[i] = -term[i] if minus else term[i]
                else:
                    into[i] = into[i] - term[i] if minus else into[i] + term[i]
    zero = jnp.zeros((SUB, LANES), jnp.float32)
    return [zero if r is None else r for r in real], [zero if m is None else m for m in imag]


def kernel(n, nx, nz, psi_ref, pot_ref, out_ref, send, recv, basis, outb, back, pots, mix,
           send_sem, recv_sem, pot_send, pot_recv, back_send, back_recv):
    me = lax.axis_index("dom")
    mesh_ids = pl.DeviceIdType.MESH
    barrier = pltpu.get_barrier_semaphore()

    def greet(k, carry):
        pl.semaphore_signal(barrier, inc=1, device_id={"dom": lax.rem(me + k, n)}, device_id_type=mesh_ids)
        return carry

    lax.fori_loop(1, n, greet, 0)

    def forward(c, here, there):
        return pltpu.make_async_remote_copy(
            src_ref=send.at[c, there], dst_ref=recv.at[c, here + 1],
            send_sem=send_sem.at[c, there], recv_sem=recv_sem.at[c, here],
            device_id={"dom": there}, device_id_type=mesh_ids)

    def pot_copy(here, there):
        return pltpu.make_async_remote_copy(
            src_ref=pot_ref, dst_ref=pots.at[here],
            send_sem=pot_send.at[there], recv_sem=pot_recv.at[here],
            device_id={"dom": there}, device_id_type=mesh_ids)

    def backward(c, here, there):
        return pltpu.make_async_remote_copy(
            src_ref=outb.at[c, there], dst_ref=back.at[c, here],
            send_sem=back_send.at[c, there], recv_sem=back_recv.at[c, here],
            device_id={"dom": there}, device_id_type=mesh_ids)

    low = lax.broadcasted_iota(jnp.int32, (n, SUB, LANES), 1) < HALF

    def interleave(a, b):
        return (jnp.where(low, a, pltpu.roll(b, HALF, 1)), jnp.where(low, pltpu.roll(a, HALF, 1), b))

    def pack(x, carry):
        parts = [psi_ref[p * nx + x].T.reshape(n, SUB, LANES) for p in range(2)]
        for c, block in enumerate(interleave(*parts)):
            send[c, :, x] = block
        return carry

    lax.fori_loop(0, nx, pack, 0)

    pots[me] = pot_ref[...]
    blank = jnp.zeros((nx, SUB, LANES), jnp.float32)
    for c in range(CHUNKS):
        recv[c, me + 1] = send[c, me]
        recv[c, 0] = blank
        recv[c, n + 1] = blank
    for j in range(ITERS - 1):
        basis[j, 0] = blank
        basis[j, n + 1] = blank

    pl.semaphore_wait(barrier, n - 1)

    def send_pot(k, carry):
        pot_copy(me, lax.rem(me + k, n)).start()
        return carry

    lax.fori_loop(1, n, send_pot, 0)
    for c in range(CHUNKS):
        def send_one(k, carry, c=c):
            forward(c, me, lax.rem(me + k, n)).start()
            return carry

        lax.fori_loop(1, n, send_one, 0)

    def wait_pot(k, carry):
        there = lax.rem(me + n - k, n)
        pot_copy(there, there).wait_recv()
        return carry

    upper = lax.broadcasted_iota(jnp.int32, (SUB, LANES), 1) >= nz
    sign = jnp.where(lax.broadcasted_iota(jnp.int32, (SUB, LANES), 0) < HALF, 1.0, -1.0)
    ratio = -0.5 * far_weight

    row = lax.broadcasted_iota(jnp.int32, (LANES, LANES), 0)
    column = lax.broadcasted_iota(jnp.int32, (LANES, LANES), 1)
    apart = lax.rem(row - column + 2 * nz, nz)
    near_z = jnp.where(jnp.logical_or(apart == 1, apart == nz - 1), 16.0, 0.0)
    far_z = jnp.where(jnp.logical_or(apart == 2, apart == nz - 2), 1.0, 0.0)
    same = (row < nz) == (column < nz)
    lanes_matrix = jnp.where(same, far_z - near_z, jnp.where(apart == 0, -16.0, 0.0)).astype(jnp.bfloat16)
    mix[0:LANES] = lanes_matrix
    mix[LANES:2 * LANES] = lanes_matrix

    def applied_at(ref, s):
        slabs = [[ref[s + g, x] for x in range(nx)] for g in range(GROUP + 2)]
        inner = jnp.concatenate([u for slab in slabs[1:-1] for u in slab], axis=0)
        high = inner.astype(jnp.bfloat16)
        rest = (inner - high.astype(jnp.float32)).astype(jnp.bfloat16)
        mixed = jnp.dot(jnp.concatenate([high, rest], axis=1), mix[...], preferred_element_type=jnp.float32)
        result = []
        for g in range(GROUP):
            before, now, after = slabs[g:g + 3]
            for x in range(nx):
                u = now[x]
                close = now[(x + 1) % nx] + now[(x - 1) % nx]
                close = close + pltpu.roll(jnp.where(upper, before[x], after[x]), nz, 1)
                wide = now[(x + 2) % nx] + now[(x - 2) % nx] + before[x] + after[x]
                at = (g * nx + x) * SUB
                wide = wide + mixed[at:at + SUB]
                own = jnp.broadcast_to(pots[s + g, pl.ds(x, 1), :], (SUB, LANES)) + -0.5 * centre_weight
                result.append((own * u + ratio * (wide - 16.0 * close), u))
        return result

    def chunk(c, carry):
        vectors = [recv.at[c]] + [basis.at[j] for j in range(ITERS - 1)]

        def arrive(k, acc):
            there = lax.rem(me + n - k, n)
            forward(c, there, there).wait_recv()
            for x in range(nx):
                u = recv[c, there + 1, x]
                acc = acc + u * u
            return acc

        acc = jnp.zeros((SUB, LANES), jnp.float32)
        for x in range(nx):
            u = recv[c, me + 1, x]
            acc = acc + u * u
        acc = lax.fori_loop(1, n, arrive, acc)
        first_norm = jnp.sqrt(total_of(acc) + epsilon)

        @pl.when(c == 0)
        def _():
            lax.fori_loop(1, n, wait_pot, 0)

        scales = [1.0 / first_norm]
        alphas, betas = [], []
        zero = jnp.zeros((SUB, LANES), jnp.float32)
        for j in range(ITERS):
            ref = vectors[j]
            last = j + 1 == ITERS
            fresh = None if last else vectors[j + 1]

            def apply(s, accs, ref=ref, fresh=fresh):
                accs = list(accs)
                for at, (w, u) in enumerate(applied_at(ref, s * GROUP)):
                    if fresh is not None:
                        fresh[s * GROUP + at // nx + 1, at % nx] = w
                    accs[at % 2] = accs[at % 2] + u * w
                return tuple(accs)

            accs = lax.fori_loop(0, n // GROUP, apply, (zero, zero), unroll=UNROLL_A)
            scale = scales[j]
            alpha = scale * (scale * total_of(accs[0] + accs[1]))
            alphas.append(alpha)
            if last:
                break
            by_self = alpha * scale
            by_previous = betas[j - 1] * scales[j - 1] if j else None

            def reduce(s, accs, ref=ref, fresh=fresh, scale=scale, by_self=by_self, by_previous=by_previous, j=j):
                accs = list(accs)
                for x in range(nx):
                    r = scale * fresh[s + 1, x] - by_self * ref[s + 1, x]
                    if j:
                        r = r - by_previous * vectors[j - 1][s + 1, x]
                    fresh[s + 1, x] = r
                    accs[x % 2] = accs[x % 2] + r * r
                return tuple(accs)

            accs = lax.fori_loop(0, n, reduce, (zero, zero), unroll=UNROLL_B)
            beta = jnp.sqrt(total_of(accs[0] + accs[1]) + epsilon)
            betas.append(beta)
            scales.append(1.0 / beta)

        real, imag = krylov_weights(alphas, betas)
        straight = [first_norm * scales[j] * real[j] for j in range(ITERS)]
        crossed = [first_norm * scales[j] * imag[j] * sign for j in range(ITERS)]

        def combined(d, x):
            us = [v[d + 1, x] for v in vectors]
            a = straight[0] * us[0]
            b = crossed[0] * us[0]
            for j in range(1, ITERS):
                a = a + straight[j] * us[j]
                b = b + crossed[j] * us[j]
            return a + swap_parts(b)

        def finish(k, carry):
            there = lax.rem(me + k, n)
            for x in range(nx):
                outb[c, there, x] = combined(there, x)

            @pl.when(k > 1)
            def _():
                backward(c, me, lax.rem(me + k - 1, n)).start()

            return carry

        lax.fori_loop(1, n, finish, 0)
        for x in range(nx):
            back[c, me, x] = combined(me, x)
        backward(c, me, lax.rem(me + n - 1, n)).start()
        return carry

    lax.fori_loop(0, CHUNKS, chunk, 0)

    for c in range(CHUNKS):
        def returned(k, carry, c=c):
            there = lax.rem(me + n - k, n)
            backward(c, there, there).wait_recv()
            return carry

        lax.fori_loop(1, n, returned, 0)

    def unpack(x, carry):
        for p, block in enumerate(interleave(back[0, :, x], back[1, :, x])):
            out_ref[p * nx + x] = block.reshape(n * SUB, LANES).T
        return carry

    lax.fori_loop(0, nx, unpack, 0)

    def sent(k, carry):
        there = lax.rem(me + k, n)
        pot_copy(me, there).wait_send()
        for c in range(CHUNKS):
            forward(c, me, there).wait_send()
            backward(c, me, there).wait_send()
        return carry

    lax.fori_loop(1, n, sent, 0)


def fused(psi, potential, n):
    parts, slabs, nx, by, nz, orbs = psi.shape
    rows = nx * by * nz // LANES
    vec = lambda *lead: pltpu.VMEM(lead + (nx, SUB, LANES), jnp.float32)
    dma = lambda *shape: pltpu.SemaphoreType.DMA(shape)
    result = pl.pallas_call(
        functools.partial(kernel, n, nx, nz),
        out_shape=jax.ShapeDtypeStruct((parts * nx, by * nz, orbs), jnp.float32),
        in_specs=[pl.BlockSpec(memory_space=pltpu.VMEM)] * 2,
        out_specs=pl.BlockSpec(memory_space=pltpu.VMEM),
        scratch_shapes=[
            vec(CHUNKS, n), vec(CHUNKS, n + 2), vec(ITERS - 1, n + 2), vec(CHUNKS, n), vec(CHUNKS, n),
            pltpu.VMEM((n, nx, LANES), jnp.float32), pltpu.VMEM((2 * LANES, LANES), jnp.bfloat16),
            dma(CHUNKS, n), dma(CHUNKS, n), dma(n), dma(n), dma(CHUNKS, n), dma(CHUNKS, n),
        ],
        compiler_params=pltpu.CompilerParams(collective_id=0, has_side_effects=True),
    )(psi.reshape(parts * nx, by * nz, orbs), potential.reshape(nx, by * nz))
    return result.reshape(psi.shape)


def fits(psi, n):
    parts, slabs, nx, by, nz, orbs = psi.shape
    return parts == 2 and slabs == 1 and by == 2 and by * nz == LANES and orbs == LANES and orbs == n * SUB and n % GROUP == 0


def per_device(n, psi, potential):
    if fits(psi, n):
        return fused(psi, potential, n)
    return on_device(psi, potential)


def solution(mesh):
    placed = (P(None, "dom", None, None, None, "st"), P("dom", None, None, None))
    return jax.shard_map(
        functools.partial(per_device, mesh.shape["dom"]),
        mesh=mesh,
        in_specs=placed,
        out_specs=P(None, "dom", None, None, None, "st"),
        check_vma=False,
    )
```

profile of v0, /device:TPU:29, one launch (start us, length us, event | category | flops | bytes accessed | tf_op | source)
XLA Modules:
  0.0 61.0 jit_solution(16181186897876224768)
XLA Ops:
  0.0 1.4 %reshape.10.pot_ref = f32[8,128]{1,0:T(8,128)} reshape(f32[1,8,2,64]{3,2,1,0:T(2,128)} %param.3) | data formatting | bytes 8192 | tf_op jit(solution)/shard_map/reshape | solution.py:411
  1.4 57.3 %shard_map.28 = f32[16,128,128]{2,1,0:T(8,128)} custom-call(f32[16,128,128]{2,1,0:T(8,128)} %bitcast.5, f32[8,128]{1,0:T(8,128)} %reshape.10.pot_ref), custom_call_target="tpu_custom_call" | custom-call | tf_op jit(solution)/shard_map/pallas_call | solution.py:400
  58.7 2.3 %copy.5 = f32[2,1,8,2,64,128]{5,4,3,2,1,0:T(8,128)} copy(f32[2,1,8,2,64,128]{5,4,3,2,1,0:T(8,128)} %bitcast.4) | data formatting | bytes 2097152
where the time goes:
time: 61.2 us; the launch traced here: 61 us
  Pallas kernels  57.3 us (94%)
  local copies, waits for them, and re-layouts  3.67 us (6%)
    pallas_call x1, Pallas kernels, fused(): pl.pallas_call(functools.partial(kernel, n, nx, nz), out_shape=jax.ShapeD...  57.3 us
    unnamed x1, local copies, waits for them, and re-layouts  2.31 us
    reshape x1, local copies, waits for them, and re-layouts, fused(): potential.reshape(nx, by * nz)  1.36 us

commit v1 on v0

--- a/solution.py
+++ b/solution.py
@@ -166,35 +166,52 @@
     return [zero if r is None else r for r in real], [zero if m is None else m for m in imag]
 
 
-def kernel(n, nx, nz, psi_ref, pot_ref, out_ref, send, recv, basis, outb, back, pots, mix,
-           send_sem, recv_sem, pot_send, pot_recv, back_send, back_recv):
+def kernel(n, nx, nz, psi_ref, pot_ref, out_ref, send, recv, extra, basis, inner, outb, outx, back, pots, mix,
+           note, heard, send_sem, recv_sem, extra_send, extra_recv, pot_send, pot_recv, back_send, back_recv,
+           far_send, note_send, note_recv):
     me = lax.axis_index("dom")
     mesh_ids = pl.DeviceIdType.MESH
     barrier = pltpu.get_barrier_semaphore()
 
+    half = n // 2
+    reach = ITERS - 1
+    deep = half - reach
+    side = me // half
+    base = side * half
+    opposite = half - base
+    partner = lax.rem(me + half, n)
+    near = half - side * reach
+    outer = jnp.logical_or(me < deep, me >= n - deep)
+
     def greet(k, carry):
         pl.semaphore_signal(barrier, inc=1, device_id={"dom": lax.rem(me + k, n)}, device_id_type=mesh_ids)
         return carry
 
     lax.fori_loop(1, n, greet, 0)
 
+    def remote(src, dst, send_to, recv_to, there):
+        return pltpu.make_async_remote_copy(
+            src_ref=src, dst_ref=dst, send_sem=send_to, recv_sem=recv_to,
+            device_id={"dom": there}, device_id_type=mesh_ids)
+
     def forward(c, here, there):
-        return pltpu.make_async_remote_copy(
-            src_ref=send.at[c, there], dst_ref=recv.at[c, here + 1],
-            send_sem=send_sem.at[c, there], recv_sem=recv_sem.at[c, here],
-            device_id={"dom": there}, device_id_type=mesh_ids)
+        return remote(send.at[c, there], recv.at[c, here + 1], send_sem.at[c], recv_sem.at[c, here], there)
+
+    def beside(c, here, there):
+        return remote(send.at[c, lax.rem(there + half, n)], extra.at[c, lax.rem(here, half) + 1],
+                      extra_send.at[c], extra_recv.at[c, lax.rem(here, half)], there)
 
     def pot_copy(here, there):
-        return pltpu.make_async_remote_copy(
-            src_ref=pot_ref, dst_ref=pots.at[here],
-            send_sem=pot_send.at[there], recv_sem=pot_recv.at[here],
-            device_id={"dom": there}, device_id_type=mesh_ids)
-
-    def backward(c, here, there):
-        return pltpu.make_async_remote_copy(
-            src_ref=outb.at[c, there], dst_ref=back.at[c, here],
-            send_sem=back_send.at[c, there], recv_sem=back_recv.at[c, here],
-            device_id={"dom": there}, device_id_type=mesh_ids)
+        return remote(pot_ref, pots.at[here], pot_send, pot_recv.at[here], there)
+
+    def backward(c, owner, there):
+        return remote(outb.at[c, there], back.at[c, owner], back_send.at[c], back_recv.at[c, owner], there)
+
+    def far_copy(c, i, there):
+        return remote(outx.at[c, i], back.at[c, partner], far_send.at[c], back_recv.at[c, partner], there)
+
+    def note_copy(c):
+        return remote(note.at[c], heard.at[c], note_send.at[c], note_recv.at[c], partner)
 
     low = lax.broadcasted_iota(jnp.int32, (n, SUB, LANES), 1) < HALF
 
@@ -215,9 +232,14 @@
         recv[c, me + 1] = send[c, me]
         recv[c, 0] = blank
         recv[c, n + 1] = blank
+        extra[c, me - base + 1] = send[c, partner]
+        extra[c, 0] = blank
+        extra[c, half + 1] = blank
     for j in range(ITERS - 1):
         basis[j, 0] = blank
         basis[j, n + 1] = blank
+        inner[j, 0] = blank
+        inner[j, half + 1] = blank
 
     pl.semaphore_wait(barrier, n - 1)
 
@@ -226,12 +248,25 @@
         return carry
 
     lax.fori_loop(1, n, send_pot, 0)
+
     for c in range(CHUNKS):
-        def send_one(k, carry, c=c):
-            forward(c, me, lax.rem(me + k, n)).start()
-            return carry
-
-        lax.fori_loop(1, n, send_one, 0)
+        def send_across(k, carry, c=c):
+            forward(c, me, opposite + lax.rem(me + k, half)).start()
+            return carry
+
+        def send_home(k, carry, c=c):
+            forward(c, me, base + lax.rem(me + k, half)).start()
+            return carry
+
+        lax.fori_loop(0, half, send_across, 0)
+        lax.fori_loop(1, half, send_home, 0)
+
+    for c in range(CHUNKS):
+        def send_beside(k, carry, c=c):
+            beside(c, me, base + lax.rem(me + k, half)).start()
+            return carry
+
+        lax.fori_loop(1, half, send_beside, 0)
 
     def wait_pot(k, carry):
         there = lax.rem(me + n - k, n)
@@ -239,6 +274,7 @@
         return carry
 
     upper = lax.broadcasted_iota(jnp.int32, (SUB, LANES), 1) >= nz
+    lane = lax.broadcasted_iota(jnp.int32, (SUB, LANES), 1)
     sign = jnp.where(lax.broadcasted_iota(jnp.int32, (SUB, LANES), 0) < HALF, 1.0, -1.0)
     ratio = -0.5 * far_weight
 
@@ -252,14 +288,14 @@
     mix[0:LANES] = lanes_matrix
     mix[LANES:2 * LANES] = lanes_matrix
 
-    def applied_at(ref, s):
-        slabs = [[ref[s + g, x] for x in range(nx)] for g in range(GROUP + 2)]
-        inner = jnp.concatenate([u for slab in slabs[1:-1] for u in slab], axis=0)
-        high = inner.astype(jnp.bfloat16)
-        rest = (inner - high.astype(jnp.float32)).astype(jnp.bfloat16)
+    def applied_at(ref, s, slab, size):
+        slabs = [[ref[s + g, x] for x in range(nx)] for g in range(size + 2)]
+        inside = jnp.concatenate([u for row_of in slabs[1:-1] for u in row_of], axis=0)
+        high = inside.astype(jnp.bfloat16)
+        rest = (inside - high.astype(jnp.float32)).astype(jnp.bfloat16)
         mixed = jnp.dot(jnp.concatenate([high, rest], axis=1), mix[...], preferred_element_type=jnp.float32)
         result = []
-        for g in range(GROUP):
+        for g in range(size):
             before, now, after = slabs[g:g + 3]
             for x in range(nx):
                 u = now[x]
@@ -268,9 +304,17 @@
                 wide = now[(x + 2) % nx] + now[(x - 2) % nx] + before[x] + after[x]
                 at = (g * nx + x) * SUB
                 wide = wide + mixed[at:at + SUB]
-                own = jnp.broadcast_to(pots[s + g, pl.ds(x, 1), :], (SUB, LANES)) + -0.5 * centre_weight
+                own = jnp.broadcast_to(pots[slab + g, pl.ds(x, 1), :], (SUB, LANES)) + -0.5 * centre_weight
                 result.append((own * u + ratio * (wide - 16.0 * close), u))
         return result
+
+    def blend(us, straight, crossed):
+        a = straight[0] * us[0]
+        b = crossed[0] * us[0]
+        for j in range(1, ITERS):
+            a = a + straight[j] * us[j]
+            b = b + crossed[j] * us[j]
+        return a + swap_parts(b)
 
     def chunk(c, carry):
         vectors = [recv.at[c]] + [basis.at[j] for j in range(ITERS - 1)]
@@ -295,7 +339,7 @@
             lax.fori_loop(1, n, wait_pot, 0)
 
         scales = [1.0 / first_norm]
-        alphas, betas = [], []
+        alphas, betas, selves, previous = [], [], [], []
         zero = jnp.zeros((SUB, LANES), jnp.float32)
         for j in range(ITERS):
             ref = vectors[j]
@@ -304,7 +348,7 @@
 
             def apply(s, accs, ref=ref, fresh=fresh):
                 accs = list(accs)
-                for at, (w, u) in enumerate(applied_at(ref, s * GROUP)):
+                for at, (w, u) in enumerate(applied_at(ref, s * GROUP, s * GROUP, GROUP)):
                     if fresh is not None:
                         fresh[s * GROUP + at // nx + 1, at % nx] = w
                     accs[at % 2] = accs[at % 2] + u * w
@@ -318,6 +362,8 @@
                 break
             by_self = alpha * scale
             by_previous = betas[j - 1] * scales[j - 1] if j else None
+            selves.append(by_self)
+            previous.append(by_previous)
 
             def reduce(s, accs, ref=ref, fresh=fresh, scale=scale, by_self=by_self, by_previous=by_previous, j=j):
                 accs = list(accs)
@@ -338,38 +384,113 @@
         straight = [first_norm * scales[j] * real[j] for j in range(ITERS)]
         crossed = [first_norm * scales[j] * imag[j] * sign for j in range(ITERS)]
 
+        told = zero
+        for k, value in enumerate(scales[:-1] + selves + previous[1:] + straight + crossed):
+            told = jnp.where(lane == k, value, told)
+        note[c] = told
+
         def combined(d, x):
-            us = [v[d + 1, x] for v in vectors]
-            a = straight[0] * us[0]
-            b = crossed[0] * us[0]
-            for j in range(1, ITERS):
-                a = a + straight[j] * us[j]
-                b = b + crossed[j] * us[j]
-            return a + swap_parts(b)
-
-        def finish(k, carry):
-            there = lax.rem(me + k, n)
+            return blend([v[d + 1, x] for v in vectors], straight, crossed)
+
+        def finish_across(k, carry):
+            there = near + lax.rem(me + k, reach)
             for x in range(nx):
                 outb[c, there, x] = combined(there, x)
 
+            @pl.when(k == 0)
+            def _():
+                note_copy(c).start()
+
+            @pl.when(k > 0)
+            def _():
+                backward(c, me, near + lax.rem(me + k - 1, reach)).start()
+
+            return carry
+
+        lax.fori_loop(0, reach, finish_across, 0)
+
+        def finish_home(k, carry):
+            there = base + lax.rem(me + k, half)
+            for x in range(nx):
+                outb[c, there, x] = combined(there, x)
+
+            @pl.when(k == 1)
+            def _():
+                backward(c, me, near + lax.rem(me + reach - 1, reach)).start()
+
             @pl.when(k > 1)
             def _():
-                backward(c, me, lax.rem(me + k - 1, n)).start()
-
-            return carry
-
-        lax.fori_loop(1, n, finish, 0)
+                backward(c, me, base + lax.rem(me + k - 1, half)).start()
+
+            return carry
+
+        lax.fori_loop(1, half, finish_home, 0)
         for x in range(nx):
             back[c, me, x] = combined(me, x)
-        backward(c, me, lax.rem(me + n - 1, n)).start()
+        backward(c, me, base + lax.rem(me + half - 1, half)).start()
+
+        def beside_arrives(k, carry):
+            there = base + lax.rem(me + k, half)
+            beside(c, there, there).wait_recv()
+            return carry
+
+        lax.fori_loop(1, half, beside_arrives, 0)
+        note_copy(c).wait_recv()
+        words = heard[c]
+        word = [jnp.broadcast_to(words[:, k:k + 1], (SUB, LANES)) for k in range(3 * reach - 1 + 2 * ITERS)]
+        scales, selves, previous = word[:reach], word[reach:2 * reach], [None] + word[2 * reach:3 * reach - 1]
+        straight, crossed = word[3 * reach - 1:3 * reach - 1 + ITERS], word[3 * reach - 1 + ITERS:]
+
+        halves = [extra.at[c]] + [inner.at[j] for j in range(reach)]
+        for j in range(reach):
+            count = half - 1 - j
+            start = (j + 1) * side
+            pieces = -(-count // GROUP)
+            at = 0
+            for piece in range(pieces):
+                size = (count - at) // (pieces - piece)
+                for i, (w, u) in enumerate(applied_at(halves[j], start + at, base + start + at, size)):
+                    here = start + at + i // nx + 1
+                    r = scales[j] * w - selves[j] * u
+                    if j:
+                        r = r - previous[j] * halves[j - 1][here, i % nx]
+                    halves[j + 1][here, i % nx] = r
+                at += size
+
+        first = reach * side
+        for i in range(deep):
+            for x in range(nx):
+                outx[c, i, x] = blend([v[first + i + 1, x] for v in halves], straight, crossed)
+        for i in range(deep):
+            there = base + first + i
+
+            @pl.when(there == me)
+            def _(i=i):
+                back[c, partner] = outx[c, i]
+
+            @pl.when(there != me)
+            def _(i=i, there=there):
+                far_copy(c, i, there).start()
         return carry
 
     lax.fori_loop(0, CHUNKS, chunk, 0)
+
+    remote(pots.at[pl.ds(0, n - 1)], pots.at[pl.ds(0, n - 1)], pot_send, pot_recv.at[0], partner).wait_send()
+    for c in range(CHUNKS):
+        blocks = send.at[c, pl.ds(0, n - 1)]
+        remote(blocks, blocks, send_sem.at[c], recv_sem.at[c, 0], partner).wait_send()
+        blocks = send.at[c, pl.ds(0, half - 1)]
+        remote(blocks, blocks, extra_send.at[c], recv_sem.at[c, 0], partner).wait_send()
+        note_copy(c).wait_send()
 
     for c in range(CHUNKS):
         def returned(k, carry, c=c):
             there = lax.rem(me + n - k, n)
-            backward(c, there, there).wait_recv()
+
+            @pl.when(jnp.logical_not(jnp.logical_and(outer, there == partner)))
+            def _():
+                backward(c, there, there).wait_recv()
+
             return carry
 
         lax.fori_loop(1, n, returned, 0)
@@ -381,21 +502,26 @@
 
     lax.fori_loop(0, nx, unpack, 0)
 
-    def sent(k, carry):
-        there = lax.rem(me + k, n)
-        pot_copy(me, there).wait_send()
-        for c in range(CHUNKS):
-            forward(c, me, there).wait_send()
-            backward(c, me, there).wait_send()
-        return carry
-
-    lax.fori_loop(1, n, sent, 0)
+    for c in range(CHUNKS):
+        blocks = outb.at[c, pl.ds(0, reach + half - 1)]
+        remote(blocks, blocks, back_send.at[c], recv_sem.at[c, 0], partner).wait_send()
+
+        @pl.when(outer)
+        def _(c=c):
+            blocks = outx.at[c, pl.ds(0, deep - 1)]
+            remote(blocks, blocks, far_send.at[c], recv_sem.at[c, 0], partner).wait_send()
+
+        @pl.when(jnp.logical_not(outer))
+        def _(c=c):
+            blocks = outx.at[c]
+            remote(blocks, blocks, far_send.at[c], recv_sem.at[c, 0], partner).wait_send()
 
 
 def fused(psi, potential, n):
     parts, slabs, nx, by, nz, orbs = psi.shape
-    rows = nx * by * nz // LANES
+    half, reach = n // 2, ITERS - 1
     vec = lambda *lead: pltpu.VMEM(lead + (nx, SUB, LANES), jnp.float32)
+    tile = lambda *lead: pltpu.VMEM(lead + (SUB, LANES), jnp.float32)
     dma = lambda *shape: pltpu.SemaphoreType.DMA(shape)
     result = pl.pallas_call(
         functools.partial(kernel, n, nx, nz),
@@ -403,9 +529,12 @@
         in_specs=[pl.BlockSpec(memory_space=pltpu.VMEM)] * 2,
         out_specs=pl.BlockSpec(memory_space=pltpu.VMEM),
         scratch_shapes=[
-            vec(CHUNKS, n), vec(CHUNKS, n + 2), vec(ITERS - 1, n + 2), vec(CHUNKS, n), vec(CHUNKS, n),
+            vec(CHUNKS, n), vec(CHUNKS, n + 2), vec(CHUNKS, half + 2), vec(reach, n + 2), vec(reach, half + 2),
+            vec(CHUNKS, n), vec(CHUNKS, half - reach), vec(CHUNKS, n),
             pltpu.VMEM((n, nx, LANES), jnp.float32), pltpu.VMEM((2 * LANES, LANES), jnp.bfloat16),
-            dma(CHUNKS, n), dma(CHUNKS, n), dma(n), dma(n), dma(CHUNKS, n), dma(CHUNKS, n),
+            tile(CHUNKS), tile(CHUNKS),
+            dma(CHUNKS), dma(CHUNKS, n), dma(CHUNKS), dma(CHUNKS, half), pltpu.SemaphoreType.DMA, dma(n),
+            dma(CHUNKS), dma(CHUNKS, n), dma(CHUNKS), dma(CHUNKS), dma(CHUNKS),
         ],
         compiler_params=pltpu.CompilerParams(collective_id=0, has_side_effects=True),
     )(psi.reshape(parts * nx, by * nz, orbs), potential.reshape(nx, by * nz))
@@ -414,7 +543,7 @@
 
 def fits(psi, n):
     parts, slabs, nx, by, nz, orbs = psi.shape
-    return parts == 2 and slabs == 1 and by == 2 and by * nz == LANES and orbs == LANES and orbs == n * SUB and n % GROUP == 0
+    return parts == 2 and slabs == 1 and by == 2 and by * nz == LANES and orbs == LANES and orbs == n * SUB and n % GROUP == 0 and n // 2 > ITERS
 
 
 def per_device(n, psi, potential):

time: 61.2 us -> 56.7 us (0.926)
  the two profiles are of different devices: /device:TPU:29 before, /device:TPU:0 now
where the time goes in v1:
time: 56.7 us; the launch traced here: 56.5 us
  Pallas kernels  52.8 us (93%)
  local copies, waits for them, and re-layouts  3.67 us (6%)
    pallas_call x1, Pallas kernels, fused(): pl.pallas_call(functools.partial(kernel, n, nx, nz), out_shape=jax.ShapeD...  52.8 us
    unnamed x1, local copies, waits for them, and re-layouts  2.31 us
    reshape x1, local copies, waits for them, and re-layouts, fused(): potential.reshape(nx, by * nz)  1.36 us

profile of v1, /device:TPU:0, one launch (start us, length us, event | category | flops | bytes accessed | tf_op | source)
XLA Modules:
  0.0 56.5 jit_solution(11146111887859192392)
XLA Ops:
  0.0 1.4 %reshape.10.pot_ref = f32[8,128]{1,0:T(8,128)} reshape(f32[1,8,2,64]{3,2,1,0:T(2,128)} %param.3) | data formatting | bytes 8192 | tf_op jit(solution)/shard_map/reshape | solution.py:540
  1.4 52.8 %shard_map.28 = f32[16,128,128]{2,1,0:T(8,128)} custom-call(f32[16,128,128]{2,1,0:T(8,128)} %bitcast.5, f32[8,128]{1,0:T(8,128)} %reshape.10.pot_ref), custom_call_target="tpu_custom_call" | custom-call | tf_op jit(solution)/shard_map/pallas_call | solution.py:526
  54.2 2.3 %copy.5 = f32[2,1,8,2,64,128]{5,4,3,2,1,0:T(8,128)} copy(f32[2,1,8,2,64,128]{5,4,3,2,1,0:T(8,128)} %bitcast.4) | data formatting | bytes 2097152

commit v2 on v1

--- a/solution.py
+++ b/solution.py
@@ -166,9 +166,30 @@
     return [zero if r is None else r for r in real], [zero if m is None else m for m in imag]
 
 
-def kernel(n, nx, nz, psi_ref, pot_ref, out_ref, send, recv, extra, basis, inner, outb, outx, back, pots, mix,
+def interleave(a, b, n):
+    low = lax.broadcasted_iota(jnp.int32, (n, SUB, LANES), 1) < HALF
+    return (jnp.where(low, a, pltpu.roll(b, HALF, 1)), jnp.where(low, pltpu.roll(a, HALF, 1), b))
+
+
+def unpack_kernel(n, nx, back, out_hbm, out, sems):
+    def put(at):
+        return pltpu.make_async_copy(out.at[at], out_hbm.at[at], sems.at[at])
+
+    for x in range(nx):
+        for p, block in enumerate(interleave(back[0, :, x], back[1, :, x], n)):
+            out[p * nx + x] = block.reshape(n * SUB, LANES).T
+        if x:
+            for p in range(2):
+                put(p * nx + x - 1).start()
+    for p in range(2):
+        put(p * nx + nx - 1).start()
+    for at in range(2 * nx):
+        put(at).wait()
+
+
+def kernel(n, nx, nz, psi_hbm, pot_hbm, back, psi_ref, pot_ref, send, recv, extra, basis, inner, outb, outx, pots, mix,
            note, heard, send_sem, recv_sem, extra_send, extra_recv, pot_send, pot_recv, back_send, back_recv,
-           far_send, note_send, note_recv):
+           far_send, note_send, note_recv, psi_sem, pot_sem):
     me = lax.axis_index("dom")
     mesh_ids = pl.DeviceIdType.MESH
     barrier = pltpu.get_barrier_semaphore()
@@ -182,12 +203,25 @@
     partner = lax.rem(me + half, n)
     near = half - side * reach
     outer = jnp.logical_or(me < deep, me >= n - deep)
+    plane = n // 4
+    spot = lax.rem(me, plane)
+    inward = jnp.logical_and(me >= plane, me < n - plane)
+    far_plane = (1 - side) * (n - plane)
 
     def greet(k, carry):
         pl.semaphore_signal(barrier, inc=1, device_id={"dom": lax.rem(me + k, n)}, device_id_type=mesh_ids)
         return carry
 
     lax.fori_loop(1, n, greet, 0)
+
+    def take_psi(at):
+        return pltpu.make_async_copy(psi_hbm.at[at], psi_ref.at[at], psi_sem.at[at])
+
+    take_pot = pltpu.make_async_copy(pot_hbm, pot_ref, pot_sem)
+    take_pot.start()
+    for x in range(nx):
+        for p in range(2):
+            take_psi(p * nx + x).start()
 
     def remote(src, dst, send_to, recv_to, there):
         return pltpu.make_async_remote_copy(
@@ -195,14 +229,14 @@
             device_id={"dom": there}, device_id_type=mesh_ids)
 
     def forward(c, here, there):
-        return remote(send.at[c, there], recv.at[c, here + 1], send_sem.at[c], recv_sem.at[c, here], there)
+        return remote(send.at[c, there], recv.at[c, here + 1], send_sem.at[c, there], recv_sem.at[c, here], there)
 
     def beside(c, here, there):
         return remote(send.at[c, lax.rem(there + half, n)], extra.at[c, lax.rem(here, half) + 1],
                       extra_send.at[c], extra_recv.at[c, lax.rem(here, half)], there)
 
     def pot_copy(here, there):
-        return remote(pot_ref, pots.at[here], pot_send, pot_recv.at[here], there)
+        return remote(pots.at[me], pots.at[here], pot_send, pot_recv.at[here], there)
 
     def backward(c, owner, there):
         return remote(outb.at[c, there], back.at[c, owner], back_send.at[c], back_recv.at[c, owner], there)
@@ -213,20 +247,18 @@
     def note_copy(c):
         return remote(note.at[c], heard.at[c], note_send.at[c], note_recv.at[c], partner)
 
-    low = lax.broadcasted_iota(jnp.int32, (n, SUB, LANES), 1) < HALF
-
-    def interleave(a, b):
-        return (jnp.where(low, a, pltpu.roll(b, HALF, 1)), jnp.where(low, pltpu.roll(a, HALF, 1), b))
-
     def pack(x, carry):
+        for p in range(2):
+            take_psi(p * nx + x).wait()
         parts = [psi_ref[p * nx + x].T.reshape(n, SUB, LANES) for p in range(2)]
-        for c, block in enumerate(interleave(*parts)):
+        for c, block in enumerate(interleave(*parts, n)):
             send[c, :, x] = block
         return carry
 
     lax.fori_loop(0, nx, pack, 0)
 
-    pots[me] = pot_ref[...]
+    take_pot.wait()
+    pots[me] = jnp.concatenate([pot_ref[:, j, :] for j in range(LANES // nz)], axis=1)
     blank = jnp.zeros((nx, SUB, LANES), jnp.float32)
     for c in range(CHUNKS):
         recv[c, me + 1] = send[c, me]
@@ -249,24 +281,46 @@
 
     lax.fori_loop(1, n, send_pot, 0)
 
-    for c in range(CHUNKS):
-        def send_across(k, carry, c=c):
-            forward(c, me, opposite + lax.rem(me + k, half)).start()
-            return carry
-
-        def send_home(k, carry, c=c):
+    def sends(c):
+        def across(k, carry):
+            there = far_plane + lax.rem(spot + k, plane)
+            forward(c, me, there).start()
+            return carry
+
+        def across_near(k, carry):
+            there = plane * (2 - side) + lax.rem(spot + k, plane)
+            forward(c, me, there).start()
+            return carry
+
+        def home(k, carry):
             forward(c, me, base + lax.rem(me + k, half)).start()
             return carry
 
-        lax.fori_loop(0, half, send_across, 0)
-        lax.fori_loop(1, half, send_home, 0)
-
-    for c in range(CHUNKS):
-        def send_beside(k, carry, c=c):
+        def cross():
+            lax.fori_loop(0, plane, across, 0)
+            lax.fori_loop(0, plane, across_near, 0)
+
+        def within():
+            lax.fori_loop(1, half, home, 0)
+
+        return cross, within
+
+    def send_beside(c):
+        def one(k, carry):
             beside(c, me, base + lax.rem(me + k, half)).start()
             return carry
 
-        lax.fori_loop(1, half, send_beside, 0)
+        lax.fori_loop(1, half, one, 0)
+
+    def first_far(k, carry):
+        there = far_plane + lax.rem(spot + k, plane)
+        forward(0, there, there).wait_recv()
+        return carry
+
+    def send_all(c):
+        cross, within = sends(c)
+        within()
+        cross()
 
     def wait_pot(k, carry):
         there = lax.rem(me + n - k, n)
@@ -316,12 +370,28 @@
             b = b + crossed[j] * us[j]
         return a + swap_parts(b)
 
+    send_all(0)
+
+    @pl.when(inward)
+    def _():
+        lax.fori_loop(0, plane, first_far, 0)
+
+    send_all(1)
+    send_beside(0)
+    send_beside(1)
+
     def chunk(c, carry):
         vectors = [recv.at[c]] + [basis.at[j] for j in range(ITERS - 1)]
 
         def arrive(k, acc):
             there = lax.rem(me + n - k, n)
-            forward(c, there, there).wait_recv()
+            early = jnp.logical_and(there >= far_plane, there < far_plane + plane)
+            early = jnp.logical_and(jnp.logical_and(inward, c == 0), early)
+
+            @pl.when(jnp.logical_not(early))
+            def _():
+                forward(c, there, there).wait_recv()
+
             for x in range(nx):
                 u = recv[c, there + 1, x]
                 acc = acc + u * u
@@ -333,6 +403,14 @@
             acc = acc + u * u
         acc = lax.fori_loop(1, n, arrive, acc)
         first_norm = jnp.sqrt(total_of(acc) + epsilon)
+
+        @pl.when(jnp.logical_and(c > 0, inward))
+        def _():
+            def held(k, carry):
+                backward(c - 1, me, near + lax.rem(me + k, reach)).start()
+                return carry
+
+            lax.fori_loop(0, reach, held, 0)
 
         @pl.when(c == 0)
         def _():
@@ -401,7 +479,7 @@
             def _():
                 note_copy(c).start()
 
-            @pl.when(k > 0)
+            @pl.when(jnp.logical_and(k > 0, jnp.logical_or(c == CHUNKS - 1, jnp.logical_not(inward))))
             def _():
                 backward(c, me, near + lax.rem(me + k - 1, reach)).start()
 
@@ -414,7 +492,7 @@
             for x in range(nx):
                 outb[c, there, x] = combined(there, x)
 
-            @pl.when(k == 1)
+            @pl.when(jnp.logical_and(k == 1, jnp.logical_or(c == CHUNKS - 1, jnp.logical_not(inward))))
             def _():
                 backward(c, me, near + lax.rem(me + reach - 1, reach)).start()
 
@@ -429,6 +507,9 @@
             back[c, me, x] = combined(me, x)
         backward(c, me, base + lax.rem(me + half - 1, half)).start()
 
+        return carry
+
+    def assist(c, carry):
         def beside_arrives(k, carry):
             there = base + lax.rem(me + k, half)
             beside(c, there, there).wait_recv()
@@ -471,14 +552,20 @@
             @pl.when(there != me)
             def _(i=i, there=there):
                 far_copy(c, i, there).start()
+
         return carry
 
     lax.fori_loop(0, CHUNKS, chunk, 0)
+    lax.fori_loop(0, CHUNKS, assist, 0)
 
     remote(pots.at[pl.ds(0, n - 1)], pots.at[pl.ds(0, n - 1)], pot_send, pot_recv.at[0], partner).wait_send()
+    def sent(k, carry):
+        for c in range(CHUNKS):
+            forward(c, me, lax.rem(me + k, n)).wait_send()
+        return carry
+
+    lax.fori_loop(1, n, sent, 0)
     for c in range(CHUNKS):
-        blocks = send.at[c, pl.ds(0, n - 1)]
-        remote(blocks, blocks, send_sem.at[c], recv_sem.at[c, 0], partner).wait_send()
         blocks = send.at[c, pl.ds(0, half - 1)]
         remote(blocks, blocks, extra_send.at[c], recv_sem.at[c, 0], partner).wait_send()
         note_copy(c).wait_send()
@@ -494,13 +581,6 @@
             return carry
 
         lax.fori_loop(1, n, returned, 0)
-
-    def unpack(x, carry):
-        for p, block in enumerate(interleave(back[0, :, x], back[1, :, x])):
-            out_ref[p * nx + x] = block.reshape(n * SUB, LANES).T
-        return carry
-
-    lax.fori_loop(0, nx, unpack, 0)
 
     for c in range(CHUNKS):
         blocks = outb.at[c, pl.ds(0, reach + half - 1)]
@@ -525,20 +605,28 @@
     dma = lambda *shape: pltpu.SemaphoreType.DMA(shape)
     result = pl.pallas_call(
         functools.partial(kernel, n, nx, nz),
-        out_shape=jax.ShapeDtypeStruct((parts * nx, by * nz, orbs), jnp.float32),
-        in_specs=[pl.BlockSpec(memory_space=pltpu.VMEM)] * 2,
+        out_shape=pltpu.VMEM((CHUNKS, n, nx, SUB, LANES), jnp.float32),
+        in_specs=[pl.BlockSpec(memory_space=pl.ANY)] * 2,
         out_specs=pl.BlockSpec(memory_space=pltpu.VMEM),
         scratch_shapes=[
+            pltpu.VMEM((parts * nx, by * nz, orbs), jnp.float32), pltpu.VMEM((nx, by, nz), jnp.float32),
             vec(CHUNKS, n), vec(CHUNKS, n + 2), vec(CHUNKS, half + 2), vec(reach, n + 2), vec(reach, half + 2),
-            vec(CHUNKS, n), vec(CHUNKS, half - reach), vec(CHUNKS, n),
+            vec(CHUNKS, n), vec(CHUNKS, half - reach),
             pltpu.VMEM((n, nx, LANES), jnp.float32), pltpu.VMEM((2 * LANES, LANES), jnp.bfloat16),
             tile(CHUNKS), tile(CHUNKS),
-            dma(CHUNKS), dma(CHUNKS, n), dma(CHUNKS), dma(CHUNKS, half), pltpu.SemaphoreType.DMA, dma(n),
-            dma(CHUNKS), dma(CHUNKS, n), dma(CHUNKS), dma(CHUNKS), dma(CHUNKS),
+            dma(CHUNKS, n), dma(CHUNKS, n), dma(CHUNKS), dma(CHUNKS, half), pltpu.SemaphoreType.DMA, dma(n),
+            dma(CHUNKS), dma(CHUNKS, n), dma(CHUNKS), dma(CHUNKS), dma(CHUNKS), dma(parts * nx), dma(),
         ],
         compiler_params=pltpu.CompilerParams(collective_id=0, has_side_effects=True),
-    )(psi.reshape(parts * nx, by * nz, orbs), potential.reshape(nx, by * nz))
-    return result.reshape(psi.shape)
+    )(psi.reshape(parts * nx, by * nz, orbs), potential.reshape(nx, by, nz))
+    out = pl.pallas_call(
+        functools.partial(unpack_kernel, n, nx),
+        out_shape=jax.ShapeDtypeStruct((parts * nx, by * nz, orbs), jnp.float32),
+        in_specs=[pl.BlockSpec(memory_space=pltpu.VMEM)],
+        out_specs=pl.BlockSpec(memory_space=pl.ANY),
+        scratch_shapes=[pltpu.VMEM((parts * nx, by * nz, orbs), jnp.float32), dma(parts * nx)],
+    )(pltpu.with_memory_space_constraint(result, pltpu.VMEM))
+    return out.reshape(psi.shape)
 
 
 def fits(psi, n):

time: 56.7 us -> 51.3 us (0.905)
  local copies, waits for them, and re-layouts: 3.67 us -> 0 us
  Pallas kernels: 52.8 us -> 51.2 us
    unnamed x1 -> x0, local copies, waits for them, and re-layouts: 2.31 us -> none
    pallas_call x1 -> x2, Pallas kernels: 52.8 us -> 51.2 us  [the longest x1 50 us: fused(): pl.pallas_call(functools.partial(kernel, n, nx, nz), out_shape=pltpu.VMEM...]
    reshape x1 -> x0, local copies, waits for them, and re-layouts: 1.36 us -> none  [fused(): potential.reshape(nx, by * nz)]
where the time goes in v2:
time: 51.3 us; the launch traced here: 51.2 us
  Pallas kernels  51.2 us (100%)
    pallas_call x1, Pallas kernels, fused(): pl.pallas_call(functools.partial(kernel, n, nx, nz), out_shape=pltpu.VMEM...  50 us
    pallas_call x1, Pallas kernels, fused(): pl.pallas_call(functools.partial(unpack_kernel, n, nx), out_shape=jax.Sha...  1.23 us

profile of v2, /device:TPU:0, one launch (start us, length us, event | category | flops | bytes accessed | tf_op | source)
XLA Modules:
  0.0 51.2 jit_solution(2766568439318746162)
XLA Ops:
  0.0 50.0 %shard_map.28.back = f32[2,16,8,8,128]{4,3,2,1,0:T(8,128)S(1)} custom-call(f32[16,128,128]{2,1,0:T(8,128)} %bitcast.5, f32[8,2,64]{2,1,0:T(2,128)} %bitcast.6), custom_call_target="tpu_custom_call" | custom-call | tf_op jit(solution)/shard_map/pallas_call | solution.py:606
  50.0 1.2 %shard_map.29 = f32[16,128,128]{2,1,0:T(8,128)} custom-call(f32[2,16,8,8,128]{4,3,2,1,0:T(8,128)S(1)} %shard_map.28.back), custom_call_target="tpu_custom_call" | custom-call | tf_op jit(solution)/shard_map/pallas_call | solution.py:622

commit v3 on v2

--- a/solution.py
+++ b/solution.py
@@ -123,8 +123,6 @@
 HALF = SUB // 2
 CHUNKS = 2
 GROUP = 4
-UNROLL_A = 4
-UNROLL_B = 8
 
 
 def swap_parts(x):
@@ -189,11 +187,12 @@
 
 def kernel(n, nx, nz, psi_hbm, pot_hbm, back, psi_ref, pot_ref, send, recv, extra, basis, inner, outb, outx, pots, mix,
            note, heard, send_sem, recv_sem, extra_send, extra_recv, pot_send, pot_recv, back_send, back_recv,
-           far_send, note_send, note_recv, psi_sem, pot_sem):
+           far_send, note_send, note_recv, psi_sem, pot_sem, held):
     me = lax.axis_index("dom")
     mesh_ids = pl.DeviceIdType.MESH
     barrier = pltpu.get_barrier_semaphore()
 
+    ratio = -0.5 * far_weight
     half = n // 2
     reach = ITERS - 1
     deep = half - reach
@@ -255,10 +254,11 @@
             send[c, :, x] = block
         return carry
 
-    lax.fori_loop(0, nx, pack, 0)
+    lax.fori_loop(0, nx, pack, 0, unroll=4)
 
     take_pot.wait()
-    pots[me] = jnp.concatenate([pot_ref[:, j, :] for j in range(LANES // nz)], axis=1)
+    pot_rows = jnp.concatenate([pot_ref[:, j, :] for j in range(LANES // nz)], axis=1)
+    pots[me] = (pot_rows + -0.5 * centre_weight) * (1.0 / ratio)
     blank = jnp.zeros((nx, SUB, LANES), jnp.float32)
     for c in range(CHUNKS):
         recv[c, me + 1] = send[c, me]
@@ -330,7 +330,6 @@
     upper = lax.broadcasted_iota(jnp.int32, (SUB, LANES), 1) >= nz
     lane = lax.broadcasted_iota(jnp.int32, (SUB, LANES), 1)
     sign = jnp.where(lax.broadcasted_iota(jnp.int32, (SUB, LANES), 0) < HALF, 1.0, -1.0)
-    ratio = -0.5 * far_weight
 
     row = lax.broadcasted_iota(jnp.int32, (LANES, LANES), 0)
     column = lax.broadcasted_iota(jnp.int32, (LANES, LANES), 1)
@@ -358,8 +357,8 @@
                 wide = now[(x + 2) % nx] + now[(x - 2) % nx] + before[x] + after[x]
                 at = (g * nx + x) * SUB
                 wide = wide + mixed[at:at + SUB]
-                own = jnp.broadcast_to(pots[slab + g, pl.ds(x, 1), :], (SUB, LANES)) + -0.5 * centre_weight
-                result.append((own * u + ratio * (wide - 16.0 * close), u))
+                own = jnp.broadcast_to(pots[slab + g, pl.ds(x, 1), :], (SUB, LANES))
+                result.append((own * u + (wide - 16.0 * close), u))
         return result
 
     def blend(us, straight, crossed):
@@ -402,68 +401,65 @@
             u = recv[c, me + 1, x]
             acc = acc + u * u
         acc = lax.fori_loop(1, n, arrive, acc)
-        first_norm = jnp.sqrt(total_of(acc) + epsilon)
+        square = total_of(acc) + epsilon
+        scale = lax.rsqrt(square)
+        first_norm = square * scale
 
         @pl.when(jnp.logical_and(c > 0, inward))
         def _():
-            def held(k, carry):
+            def kept(k, carry):
                 backward(c - 1, me, near + lax.rem(me + k, reach)).start()
                 return carry
 
-            lax.fori_loop(0, reach, held, 0)
+            del kept
 
         @pl.when(c == 0)
         def _():
             lax.fori_loop(1, n, wait_pot, 0)
 
-        scales = [1.0 / first_norm]
+        scales, steps = [scale], []
         alphas, betas, selves, previous = [], [], [], []
         zero = jnp.zeros((SUB, LANES), jnp.float32)
         for j in range(ITERS):
             ref = vectors[j]
-            last = j + 1 == ITERS
-            fresh = None if last else vectors[j + 1]
-
-            def apply(s, accs, ref=ref, fresh=fresh):
-                accs = list(accs)
-                for at, (w, u) in enumerate(applied_at(ref, s * GROUP, s * GROUP, GROUP)):
-                    if fresh is not None:
-                        fresh[s * GROUP + at // nx + 1, at % nx] = w
-                    accs[at % 2] = accs[at % 2] + u * w
-                return tuple(accs)
-
-            accs = lax.fori_loop(0, n // GROUP, apply, (zero, zero), unroll=UNROLL_A)
-            scale = scales[j]
-            alpha = scale * (scale * total_of(accs[0] + accs[1]))
+            products = [zero, zero]
+            squares = [zero, zero]
+            done = 0
+            for g in range(n // GROUP + 1):
+                if j and g < n // GROUP:
+                    for s in range(g * GROUP, (g + 1) * GROUP):
+                        for x in range(nx):
+                            r = steps[-1] * held[(j - 1) % 2, s, x] - selves[-1] * vectors[j - 1][s + 1, x]
+                            if j > 1:
+                                r = r - previous[-1] * vectors[j - 2][s + 1, x]
+                            ref[s + 1, x] = r
+                            squares[x % 2] = squares[x % 2] + r * r
+                if j and g == n // GROUP:
+                    square = total_of(squares[0] + squares[1]) + epsilon
+                upto = n if g == n // GROUP else (g + 1) * GROUP - 1
+                for at, (w, u) in enumerate(applied_at(ref, done, done, upto - done)):
+                    if j + 1 < ITERS:
+                        held[j % 2, done + at // nx, at % nx] = w
+                    products[at % 2] = products[at % 2] + u * w
+                done = upto
+            if j:
+                scale = lax.rsqrt(square)
+                scales.append(scale)
+                betas.append(square * scale)
+            step = scale * ratio
+            alpha = step * (scale * total_of(products[0] + products[1]))
             alphas.append(alpha)
-            if last:
-                break
-            by_self = alpha * scale
-            by_previous = betas[j - 1] * scales[j - 1] if j else None
-            selves.append(by_self)
-            previous.append(by_previous)
-
-            def reduce(s, accs, ref=ref, fresh=fresh, scale=scale, by_self=by_self, by_previous=by_previous, j=j):
-                accs = list(accs)
-                for x in range(nx):
-                    r = scale * fresh[s + 1, x] - by_self * ref[s + 1, x]
-                    if j:
-                        r = r - by_previous * vectors[j - 1][s + 1, x]
-                    fresh[s + 1, x] = r
-                    accs[x % 2] = accs[x % 2] + r * r
-                return tuple(accs)
-
-            accs = lax.fori_loop(0, n, reduce, (zero, zero), unroll=UNROLL_B)
-            beta = jnp.sqrt(total_of(accs[0] + accs[1]) + epsilon)
-            betas.append(beta)
-            scales.append(1.0 / beta)
+            if j + 1 < ITERS:
+                steps.append(step)
+                selves.append(alpha * scale)
+                previous.append(betas[-1] * scales[-2] if j else None)
 
         real, imag = krylov_weights(alphas, betas)
         straight = [first_norm * scales[j] * real[j] for j in range(ITERS)]
         crossed = [first_norm * scales[j] * imag[j] * sign for j in range(ITERS)]
 
         told = zero
-        for k, value in enumerate(scales[:-1] + selves + previous[1:] + straight + crossed):
+        for k, value in enumerate(steps + selves + previous[1:] + straight + crossed):
             told = jnp.where(lane == k, value, told)
         note[c] = told
 
@@ -479,6 +475,14 @@
             def _():
                 note_copy(c).start()
 
+            @pl.when(jnp.logical_and(k == 1, jnp.logical_and(c > 0, inward)))
+            def _():
+                def late(i, carry):
+                    backward(c - 1, me, near + lax.rem(me + i, reach)).start()
+                    return carry
+
+                lax.fori_loop(0, reach, late, 0)
+
             @pl.when(jnp.logical_and(k > 0, jnp.logical_or(c == CHUNKS - 1, jnp.logical_not(inward))))
             def _():
                 backward(c, me, near + lax.rem(me + k - 1, reach)).start()
@@ -519,7 +523,7 @@
         note_copy(c).wait_recv()
         words = heard[c]
         word = [jnp.broadcast_to(words[:, k:k + 1], (SUB, LANES)) for k in range(3 * reach - 1 + 2 * ITERS)]
-        scales, selves, previous = word[:reach], word[reach:2 * reach], [None] + word[2 * reach:3 * reach - 1]
+        steps, selves, previous = word[:reach], word[reach:2 * reach], [None] + word[2 * reach:3 * reach - 1]
         straight, crossed = word[3 * reach - 1:3 * reach - 1 + ITERS], word[3 * reach - 1 + ITERS:]
 
         halves = [extra.at[c]] + [inner.at[j] for j in range(reach)]
@@ -532,7 +536,7 @@
                 size = (count - at) // (pieces - piece)
                 for i, (w, u) in enumerate(applied_at(halves[j], start + at, base + start + at, size)):
                     here = start + at + i // nx + 1
-                    r = scales[j] * w - selves[j] * u
+                    r = steps[j] * w - selves[j] * u
                     if j:
                         r = r - previous[j] * halves[j - 1][here, i % nx]
                     halves[j + 1][here, i % nx] = r
@@ -615,7 +619,7 @@
             pltpu.VMEM((n, nx, LANES), jnp.float32), pltpu.VMEM((2 * LANES, LANES), jnp.bfloat16),
             tile(CHUNKS), tile(CHUNKS),
             dma(CHUNKS, n), dma(CHUNKS, n), dma(CHUNKS), dma(CHUNKS, half), pltpu.SemaphoreType.DMA, dma(n),
-            dma(CHUNKS), dma(CHUNKS, n), dma(CHUNKS), dma(CHUNKS), dma(CHUNKS), dma(parts * nx), dma(),
+            dma(CHUNKS), dma(CHUNKS, n), dma(CHUNKS), dma(CHUNKS), dma(CHUNKS), dma(parts * nx), dma(), vec(2, n),
         ],
         compiler_params=pltpu.CompilerParams(collective_id=0, has_side_effects=True),
     )(psi.reshape(parts * nx, by * nz, orbs), potential.reshape(nx, by, nz))

time: 51.3 us -> 49.7 us (0.969)
  Pallas kernels: 51.2 us -> 49.6 us
    pallas_call x1, Pallas kernels: 50 us -> 48.3 us  [fused(): pl.pallas_call(functools.partial(kernel, n, nx, nz), out_shape=pltpu.VMEM...]
where the time goes in v3:
time: 49.7 us; the launch traced here: 49.6 us
  Pallas kernels  49.6 us (100%)
    pallas_call x1, Pallas kernels, fused(): pl.pallas_call(functools.partial(kernel, n, nx, nz), out_shape=pltpu.VMEM...  48.3 us
    pallas_call x1, Pallas kernels, fused(): pl.pallas_call(functools.partial(unpack_kernel, n, nx), out_shape=jax.Sha...  1.23 us

profile of v3, /device:TPU:0, one launch (start us, length us, event | category | flops | bytes accessed | tf_op | source)
XLA Modules:
  0.0 49.6 jit_solution(6841128466511127689)
XLA Ops:
  0.0 48.3 %shard_map.28.back = f32[2,16,8,8,128]{4,3,2,1,0:T(8,128)S(1)} custom-call(f32[16,128,128]{2,1,0:T(8,128)} %bitcast.5, f32[8,2,64]{2,1,0:T(2,128)} %bitcast.6), custom_call_target="tpu_custom_call" | custom-call | tf_op jit(solution)/shard_map/pallas_call | solution.py:610
  48.3 1.2 %shard_map.29 = f32[16,128,128]{2,1,0:T(8,128)} custom-call(f32[2,16,8,8,128]{4,3,2,1,0:T(8,128)S(1)} %shard_map.28.back), custom_call_target="tpu_custom_call" | custom-call | tf_op jit(solution)/shard_map/pallas_call | solution.py:626

commit v4 on v3

--- a/solution.py
+++ b/solution.py
@@ -169,20 +169,17 @@
     return (jnp.where(low, a, pltpu.roll(b, HALF, 1)), jnp.where(low, pltpu.roll(a, HALF, 1), b))
 
 
-def unpack_kernel(n, nx, back, out_hbm, out, sems):
-    def put(at):
-        return pltpu.make_async_copy(out.at[at], out_hbm.at[at], sems.at[at])
+def unpack_kernel(n, nx, back, out_hbm, out, sem):
+    def put(x):
+        return pltpu.make_async_copy(out.at[:, x], out_hbm.at[:, x], sem)
 
     for x in range(nx):
         for p, block in enumerate(interleave(back[0, :, x], back[1, :, x], n)):
-            out[p * nx + x] = block.reshape(n * SUB, LANES).T
+            out[p, x] = block.reshape(n * SUB, LANES).T
         if x:
-            for p in range(2):
-                put(p * nx + x - 1).start()
-    for p in range(2):
-        put(p * nx + nx - 1).start()
-    for at in range(2 * nx):
-        put(at).wait()
+            put(x - 1).start()
+    put(nx - 1).start()
+    pltpu.make_async_copy(out, out_hbm, sem).wait()
 
 
 def kernel(n, nx, nz, psi_hbm, pot_hbm, back, psi_ref, pot_ref, send, recv, extra, basis, inner, outb, outx, pots, mix,
@@ -213,14 +210,13 @@
 
     lax.fori_loop(1, n, greet, 0)
 
-    def take_psi(at):
-        return pltpu.make_async_copy(psi_hbm.at[at], psi_ref.at[at], psi_sem.at[at])
+    def take_psi(x):
+        return pltpu.make_async_copy(psi_hbm.at[:, x], psi_ref.at[:, x], psi_sem.at[x])
 
     take_pot = pltpu.make_async_copy(pot_hbm, pot_ref, pot_sem)
     take_pot.start()
     for x in range(nx):
-        for p in range(2):
-            take_psi(p * nx + x).start()
+        take_psi(x).start()
 
     def remote(src, dst, send_to, recv_to, there):
         return pltpu.make_async_remote_copy(
@@ -228,28 +224,27 @@
             device_id={"dom": there}, device_id_type=mesh_ids)
 
     def forward(c, here, there):
-        return remote(send.at[c, there], recv.at[c, here + 1], send_sem.at[c, there], recv_sem.at[c, here], there)
+        return remote(send.at[c, there], recv.at[c, here + 1], send_sem.at[c], recv_sem.at[c, here // plane], there)
 
     def beside(c, here, there):
         return remote(send.at[c, lax.rem(there + half, n)], extra.at[c, lax.rem(here, half) + 1],
-                      extra_send.at[c], extra_recv.at[c, lax.rem(here, half)], there)
+                      extra_send.at[c], extra_recv.at[c], there)
 
     def pot_copy(here, there):
-        return remote(pots.at[me], pots.at[here], pot_send, pot_recv.at[here], there)
+        return remote(pots.at[me], pots.at[here], pot_send, pot_recv, there)
 
     def backward(c, owner, there):
-        return remote(outb.at[c, there], back.at[c, owner], back_send.at[c], back_recv.at[c, owner], there)
+        return remote(outb.at[c, there], back.at[c, owner], back_send.at[c], back_recv.at[c], there)
 
     def far_copy(c, i, there):
-        return remote(outx.at[c, i], back.at[c, partner], far_send.at[c], back_recv.at[c, partner], there)
+        return remote(outx.at[c, i], back.at[c, partner], far_send.at[c], back_recv.at[c], there)
 
     def note_copy(c):
         return remote(note.at[c], heard.at[c], note_send.at[c], note_recv.at[c], partner)
 
     def pack(x, carry):
-        for p in range(2):
-            take_psi(p * nx + x).wait()
-        parts = [psi_ref[p * nx + x].T.reshape(n, SUB, LANES) for p in range(2)]
+        take_psi(x).wait()
+        parts = [psi_ref[p, x].T.reshape(n, SUB, LANES) for p in range(2)]
         for c, block in enumerate(interleave(*parts, n)):
             send[c, :, x] = block
         return carry
@@ -312,20 +307,16 @@
 
         lax.fori_loop(1, half, one, 0)
 
-    def first_far(k, carry):
-        there = far_plane + lax.rem(spot + k, plane)
-        forward(0, there, there).wait_recv()
-        return carry
+    def landed(blocks, arrived):
+        remote(blocks, blocks, note_send.at[0], arrived, partner).wait_recv()
+
+    def left(blocks, departed):
+        remote(blocks, blocks, departed, note_recv.at[0], partner).wait_send()
 
     def send_all(c):
         cross, within = sends(c)
         within()
         cross()
-
-    def wait_pot(k, carry):
-        there = lax.rem(me + n - k, n)
-        pot_copy(there, there).wait_recv()
-        return carry
 
     upper = lax.broadcasted_iota(jnp.int32, (SUB, LANES), 1) >= nz
     lane = lax.broadcasted_iota(jnp.int32, (SUB, LANES), 1)
@@ -373,7 +364,7 @@
 
     @pl.when(inward)
     def _():
-        lax.fori_loop(0, plane, first_far, 0)
+        landed(recv.at[0, pl.ds(0, plane)], recv_sem.at[0, far_plane // plane])
 
     send_all(1)
     send_beside(0)
@@ -382,25 +373,27 @@
     def chunk(c, carry):
         vectors = [recv.at[c]] + [basis.at[j] for j in range(ITERS - 1)]
 
-        def arrive(k, acc):
-            there = lax.rem(me + n - k, n)
-            early = jnp.logical_and(there >= far_plane, there < far_plane + plane)
-            early = jnp.logical_and(jnp.logical_and(inward, c == 0), early)
-
-            @pl.when(jnp.logical_not(early))
-            def _():
-                forward(c, there, there).wait_recv()
-
-            for x in range(nx):
-                u = recv[c, there + 1, x]
-                acc = acc + u * u
-            return acc
-
+        own = me // plane * plane
+        beyond = base + lax.rem(me - base + plane, half) // plane * plane
+        across = plane * (2 - side)
         acc = jnp.zeros((SUB, LANES), jnp.float32)
-        for x in range(nx):
-            u = recv[c, me + 1, x]
-            acc = acc + u * u
-        acc = lax.fori_loop(1, n, arrive, acc)
+        for first, count in ((own, plane - 1), (beyond, plane), (across, plane), (far_plane, plane)):
+            blocks = recv.at[c, pl.ds(0, count)]
+            arrived = recv_sem.at[c, first // plane]
+            if first is far_plane:
+                @pl.when(jnp.logical_not(jnp.logical_and(inward, c == 0)))
+                def _(blocks=blocks, arrived=arrived):
+                    landed(blocks, arrived)
+            else:
+                landed(blocks, arrived)
+
+            def sum_up(k, acc, first=first):
+                for x in range(nx):
+                    u = recv[c, first + k + 1, x]
+                    acc = acc + u * u
+                return acc
+
+            acc = lax.fori_loop(0, plane, sum_up, acc, unroll=True)
         square = total_of(acc) + epsilon
         scale = lax.rsqrt(square)
         first_norm = square * scale
@@ -415,7 +408,7 @@
 
         @pl.when(c == 0)
         def _():
-            lax.fori_loop(1, n, wait_pot, 0)
+            landed(pots.at[pl.ds(0, n - 1)], pot_recv)
 
         scales, steps = [scale], []
         alphas, betas, selves, previous = [], [], [], []
@@ -514,12 +507,7 @@
         return carry
 
     def assist(c, carry):
-        def beside_arrives(k, carry):
-            there = base + lax.rem(me + k, half)
-            beside(c, there, there).wait_recv()
-            return carry
-
-        lax.fori_loop(1, half, beside_arrives, 0)
+        landed(extra.at[c, pl.ds(0, half - 1)], extra_recv.at[c])
         note_copy(c).wait_recv()
         words = heard[c]
         word = [jnp.broadcast_to(words[:, k:k + 1], (SUB, LANES)) for k in range(3 * reach - 1 + 2 * ITERS)]
@@ -562,43 +550,21 @@
     lax.fori_loop(0, CHUNKS, chunk, 0)
     lax.fori_loop(0, CHUNKS, assist, 0)
 
-    remote(pots.at[pl.ds(0, n - 1)], pots.at[pl.ds(0, n - 1)], pot_send, pot_recv.at[0], partner).wait_send()
-    def sent(k, carry):
-        for c in range(CHUNKS):
-            forward(c, me, lax.rem(me + k, n)).wait_send()
-        return carry
-
-    lax.fori_loop(1, n, sent, 0)
+    left(pots.at[pl.ds(0, n - 1)], pot_send)
     for c in range(CHUNKS):
-        blocks = send.at[c, pl.ds(0, half - 1)]
-        remote(blocks, blocks, extra_send.at[c], recv_sem.at[c, 0], partner).wait_send()
+        left(send.at[c, pl.ds(0, n - 1)], send_sem.at[c])
+        left(send.at[c, pl.ds(0, half - 1)], extra_send.at[c])
         note_copy(c).wait_send()
 
+    for mine, count in ((outer, n - 2), (jnp.logical_not(outer), n - 1)):
+        @pl.when(mine)
+        def _(count=count):
+            for c in range(CHUNKS):
+                landed(back.at[c, pl.ds(0, count)], back_recv.at[c])
+                left(outx.at[c, pl.ds(0, count - n + 1 + deep)], far_send.at[c])
+
     for c in range(CHUNKS):
-        def returned(k, carry, c=c):
-            there = lax.rem(me + n - k, n)
-
-            @pl.when(jnp.logical_not(jnp.logical_and(outer, there == partner)))
-            def _():
-                backward(c, there, there).wait_recv()
-
-            return carry
-
-        lax.fori_loop(1, n, returned, 0)
-
-    for c in range(CHUNKS):
-        blocks = outb.at[c, pl.ds(0, reach + half - 1)]
-        remote(blocks, blocks, back_send.at[c], recv_sem.at[c, 0], partner).wait_send()
-
-        @pl.when(outer)
-        def _(c=c):
-            blocks = outx.at[c, pl.ds(0, deep - 1)]
-            remote(blocks, blocks, far_send.at[c], recv_sem.at[c, 0], partner).wait_send()
-
-        @pl.when(jnp.logical_not(outer))
-        def _(c=c):
-            blocks = outx.at[c]
-            remote(blocks, blocks, far_send.at[c], recv_sem.at[c, 0], partner).wait_send()
+        left(outb.at[c, pl.ds(0, reach + half - 1)], back_send.at[c])
 
 
 def fused(psi, potential, n):
@@ -613,22 +579,22 @@
         in_specs=[pl.BlockSpec(memory_space=pl.ANY)] * 2,
         out_specs=pl.BlockSpec(memory_space=pltpu.VMEM),
         scratch_shapes=[
-            pltpu.VMEM((parts * nx, by * nz, orbs), jnp.float32), pltpu.VMEM((nx, by, nz), jnp.float32),
+            pltpu.VMEM((parts, nx, by * nz, orbs), jnp.float32), pltpu.VMEM((nx, by, nz), jnp.float32),
             vec(CHUNKS, n), vec(CHUNKS, n + 2), vec(CHUNKS, half + 2), vec(reach, n + 2), vec(reach, half + 2),
             vec(CHUNKS, n), vec(CHUNKS, half - reach),
             pltpu.VMEM((n, nx, LANES), jnp.float32), pltpu.VMEM((2 * LANES, LANES), jnp.bfloat16),
             tile(CHUNKS), tile(CHUNKS),
-            dma(CHUNKS, n), dma(CHUNKS, n), dma(CHUNKS), dma(CHUNKS, half), pltpu.SemaphoreType.DMA, dma(n),
-            dma(CHUNKS), dma(CHUNKS, n), dma(CHUNKS), dma(CHUNKS), dma(CHUNKS), dma(parts * nx), dma(), vec(2, n),
+            dma(CHUNKS), dma(CHUNKS, 4), dma(CHUNKS), dma(CHUNKS), dma(), dma(),
+            dma(CHUNKS), dma(CHUNKS), dma(CHUNKS), dma(CHUNKS), dma(CHUNKS), dma(nx), dma(), vec(2, n),
         ],
         compiler_params=pltpu.CompilerParams(collective_id=0, has_side_effects=True),
-    )(psi.reshape(parts * nx, by * nz, orbs), potential.reshape(nx, by, nz))
+    )(psi.reshape(parts, nx, by * nz, orbs), potential.reshape(nx, by, nz))
     out = pl.pallas_call(
         functools.partial(unpack_kernel, n, nx),
-        out_shape=jax.ShapeDtypeStruct((parts * nx, by * nz, orbs), jnp.float32),
+        out_shape=jax.ShapeDtypeStruct((parts, nx, by * nz, orbs), jnp.float32),
         in_specs=[pl.BlockSpec(memory_space=pltpu.VMEM)],
         out_specs=pl.BlockSpec(memory_space=pl.ANY),
-        scratch_shapes=[pltpu.VMEM((parts * nx, by * nz, orbs), jnp.float32), dma(parts * nx)],
+        scratch_shapes=[pltpu.VMEM((parts, nx, by * nz, orbs), jnp.float32), dma()],
     )(pltpu.with_memory_space_constraint(result, pltpu.VMEM))
     return out.reshape(psi.shape)
 

time: 49.7 us -> 48.5 us (0.976)
  Pallas kernels: 49.6 us -> 48.3 us
    pallas_call x1, Pallas kernels: 48.3 us -> 47.2 us  [fused(): pl.pallas_call(functools.partial(kernel, n, nx, nz), out_shape=pltpu.VMEM...]
where the time goes in v4:
time: 48.5 us; the launch traced here: 48.3 us
  Pallas kernels  48.3 us (100%)
    pallas_call x1, Pallas kernels, fused(): pl.pallas_call(functools.partial(kernel, n, nx, nz), out_shape=pltpu.VMEM...  47.2 us
    pallas_call x1, Pallas kernels, fused(): pl.pallas_call(functools.partial(unpack_kernel, n, nx), out_shape=jax.Sha...  1.1 us

profile of v4, /device:TPU:0, one launch (start us, length us, event | category | flops | bytes accessed | tf_op | source)
XLA Modules:
  0.0 48.3 jit_solution(17881484696220524490)
XLA Ops:
  0.0 47.2 %shard_map.28.back = f32[2,16,8,8,128]{4,3,2,1,0:T(8,128)S(1)} custom-call(f32[2,8,128,128]{3,2,1,0:T(8,128)} %bitcast.5, f32[8,2,64]{2,1,0:T(2,128)} %bitcast.6), custom_call_target="tpu_custom_call" | custom-call | tf_op jit(solution)/shard_map/pallas_call | solution.py:576
  47.2 1.1 %shard_map.29 = f32[2,8,128,128]{3,2,1,0:T(8,128)} custom-call(f32[2,16,8,8,128]{4,3,2,1,0:T(8,128)S(1)} %shard_map.28.back), custom_call_target="tpu_custom_call" | custom-call | tf_op jit(solution)/shard_map/pallas_call | solution.py:592

commit v5 on v4

--- a/solution.py
+++ b/solution.py
@@ -203,6 +203,7 @@
     spot = lax.rem(me, plane)
     inward = jnp.logical_and(me >= plane, me < n - plane)
     far_plane = (1 - side) * (n - plane)
+    outward = jnp.logical_not(inward)
 
     def greet(k, carry):
         pl.semaphore_signal(barrier, inc=1, device_id={"dom": lax.rem(me + k, n)}, device_id_type=mesh_ids)
@@ -276,29 +277,33 @@
 
     lax.fori_loop(1, n, send_pot, 0)
 
-    def sends(c):
-        def across(k, carry):
-            there = far_plane + lax.rem(spot + k, plane)
-            forward(c, me, there).start()
+    def send_far(c):
+        def one(k, carry):
+            forward(c, me, far_plane + lax.rem(spot + k, plane)).start()
             return carry
 
-        def across_near(k, carry):
-            there = plane * (2 - side) + lax.rem(spot + k, plane)
-            forward(c, me, there).start()
+        lax.fori_loop(0, plane, one, 0)
+
+    def send_near(c):
+        def one(k, carry):
+            forward(c, me, plane * (2 - side) + lax.rem(spot + k, plane)).start()
             return carry
 
-        def home(k, carry):
-            forward(c, me, base + lax.rem(me + k, half)).start()
+        lax.fori_loop(0, plane, one, 0)
+
+    def send_plane(c):
+        def one(k, carry):
+            forward(c, me, me - spot + lax.rem(spot + k, plane)).start()
             return carry
 
-        def cross():
-            lax.fori_loop(0, plane, across, 0)
-            lax.fori_loop(0, plane, across_near, 0)
-
-        def within():
-            lax.fori_loop(1, half, home, 0)
-
-        return cross, within
+        lax.fori_loop(1, plane, one, 0)
+
+    def send_next(c):
+        def one(k, carry):
+            forward(c, me, base + lax.rem(me - spot - base + plane, half) + lax.rem(spot + k, plane)).start()
+            return carry
+
+        lax.fori_loop(0, plane, one, 0)
 
     def send_beside(c):
         def one(k, carry):
@@ -312,11 +317,6 @@
 
     def left(blocks, departed):
         remote(blocks, blocks, departed, note_recv.at[0], partner).wait_send()
-
-    def send_all(c):
-        cross, within = sends(c)
-        within()
-        cross()
 
     upper = lax.broadcasted_iota(jnp.int32, (SUB, LANES), 1) >= nz
     lane = lax.broadcasted_iota(jnp.int32, (SUB, LANES), 1)
@@ -360,15 +360,32 @@
             b = b + crossed[j] * us[j]
         return a + swap_parts(b)
 
-    send_all(0)
+    @pl.when(outward)
+    def _():
+        send_next(0)
+        send_plane(0)
+        send_far(0)
+        send_near(0)
+        send_next(1)
+        send_plane(1)
+        send_far(1)
+        send_near(1)
+        send_beside(0)
+        send_beside(1)
 
     @pl.when(inward)
     def _():
+        send_plane(0)
+        send_near(0)
+        send_far(0)
+        send_next(0)
+        send_next(1)
+        send_plane(1)
+        send_beside(0)
+        send_beside(1)
         landed(recv.at[0, pl.ds(0, plane)], recv_sem.at[0, far_plane // plane])
-
-    send_all(1)
-    send_beside(0)
-    send_beside(1)
+        send_near(1)
+        send_far(1)
 
     def chunk(c, carry):
         vectors = [recv.at[c]] + [basis.at[j] for j in range(ITERS - 1)]
@@ -397,14 +414,6 @@
         square = total_of(acc) + epsilon
         scale = lax.rsqrt(square)
         first_norm = square * scale
-
-        @pl.when(jnp.logical_and(c > 0, inward))
-        def _():
-            def kept(k, carry):
-                backward(c - 1, me, near + lax.rem(me + k, reach)).start()
-                return carry
-
-            del kept
 
         @pl.when(c == 0)
         def _():

time: 48.5 us -> 47.8 us (0.986)
  Pallas kernels: 48.3 us -> 47.6 us
    pallas_call x1, Pallas kernels: 47.2 us -> 46.5 us  [fused(): pl.pallas_call(functools.partial(kernel, n, nx, nz), out_shape=pltpu.VMEM...]
where the time goes in v5:
time: 47.8 us; the launch traced here: 47.6 us
  Pallas kernels  47.6 us (100%)
    pallas_call x1, Pallas kernels, fused(): pl.pallas_call(functools.partial(kernel, n, nx, nz), out_shape=pltpu.VMEM...  46.5 us
    pallas_call x1, Pallas kernels, fused(): pl.pallas_call(functools.partial(unpack_kernel, n, nx), out_shape=jax.Sha...  1.1 us

profile of v5, /device:TPU:0, one launch (start us, length us, event | category | flops | bytes accessed | tf_op | source)
XLA Modules:
  0.0 47.6 jit_solution(9412117279901625634)
XLA Ops:
  0.0 46.5 %shard_map.28.back = f32[2,16,8,8,128]{4,3,2,1,0:T(8,128)S(1)} custom-call(f32[2,8,128,128]{3,2,1,0:T(8,128)} %bitcast.5, f32[8,2,64]{2,1,0:T(2,128)} %bitcast.6), custom_call_target="tpu_custom_call" | custom-call | tf_op jit(solution)/shard_map/pallas_call | solution.py:585
  46.5 1.1 %shard_map.29 = f32[2,8,128,128]{3,2,1,0:T(8,128)} custom-call(f32[2,16,8,8,128]{4,3,2,1,0:T(8,128)S(1)} %shard_map.28.back), custom_call_target="tpu_custom_call" | custom-call | tf_op jit(solution)/shard_map/pallas_call | solution.py:601

commit v6 on v5

--- a/solution.py
+++ b/solution.py
@@ -212,11 +212,12 @@
     lax.fori_loop(1, n, greet, 0)
 
     def take_psi(x):
-        return pltpu.make_async_copy(psi_hbm.at[:, x], psi_ref.at[:, x], psi_sem.at[x])
+        part = pl.ds(x * (nx // 2), nx // 2)
+        return pltpu.make_async_copy(psi_hbm.at[:, part], psi_ref.at[:, part], psi_sem.at[x])
 
     take_pot = pltpu.make_async_copy(pot_hbm, pot_ref, pot_sem)
     take_pot.start()
-    for x in range(nx):
+    for x in range(2):
         take_psi(x).start()
 
     def remote(src, dst, send_to, recv_to, there):
@@ -225,32 +226,33 @@
             device_id={"dom": there}, device_id_type=mesh_ids)
 
     def forward(c, here, there):
-        return remote(send.at[c, there], recv.at[c, here + 1], send_sem.at[c], recv_sem.at[c, here // plane], there)
+        return remote(send.at[c, there], recv.at[c, here + 1], send_sem, recv_sem.at[c, here // plane], there)
 
     def beside(c, here, there):
         return remote(send.at[c, lax.rem(there + half, n)], extra.at[c, lax.rem(here, half) + 1],
-                      extra_send.at[c], extra_recv.at[c], there)
+                      extra_send, extra_recv.at[c], there)
 
     def pot_copy(here, there):
         return remote(pots.at[me], pots.at[here], pot_send, pot_recv, there)
 
     def backward(c, owner, there):
-        return remote(outb.at[c, there], back.at[c, owner], back_send.at[c], back_recv.at[c], there)
+        return remote(outb.at[c, there], back.at[c, owner], back_send, back_recv.at[c], there)
 
     def far_copy(c, i, there):
-        return remote(outx.at[c, i], back.at[c, partner], far_send.at[c], back_recv.at[c], there)
+        return remote(outx.at[c, i], back.at[c, partner], far_send, back_recv.at[c], there)
 
     def note_copy(c):
-        return remote(note.at[c], heard.at[c], note_send.at[c], note_recv.at[c], partner)
+        return remote(note.at[c], heard.at[c], note_send, note_recv.at[c], partner)
 
     def pack(x, carry):
-        take_psi(x).wait()
         parts = [psi_ref[p, x].T.reshape(n, SUB, LANES) for p in range(2)]
         for c, block in enumerate(interleave(*parts, n)):
             send[c, :, x] = block
         return carry
 
-    lax.fori_loop(0, nx, pack, 0, unroll=4)
+    for x in range(2):
+        take_psi(x).wait()
+        lax.fori_loop(x * (nx // 2), (x + 1) * (nx // 2), pack, 0, unroll=True)
 
     take_pot.wait()
     pot_rows = jnp.concatenate([pot_ref[:, j, :] for j in range(LANES // nz)], axis=1)
@@ -313,7 +315,7 @@
         lax.fori_loop(1, half, one, 0)
 
     def landed(blocks, arrived):
-        remote(blocks, blocks, note_send.at[0], arrived, partner).wait_recv()
+        remote(blocks, blocks, note_send, arrived, partner).wait_recv()
 
     def left(blocks, departed):
         remote(blocks, blocks, departed, note_recv.at[0], partner).wait_send()
@@ -560,20 +562,18 @@
     lax.fori_loop(0, CHUNKS, assist, 0)
 
     left(pots.at[pl.ds(0, n - 1)], pot_send)
-    for c in range(CHUNKS):
-        left(send.at[c, pl.ds(0, n - 1)], send_sem.at[c])
-        left(send.at[c, pl.ds(0, half - 1)], extra_send.at[c])
-        note_copy(c).wait_send()
+    left(send.at[:, pl.ds(0, n - 1)], send_sem)
+    left(send.at[:, pl.ds(0, half - 1)], extra_send)
+    left(note, note_send)
 
     for mine, count in ((outer, n - 2), (jnp.logical_not(outer), n - 1)):
         @pl.when(mine)
         def _(count=count):
             for c in range(CHUNKS):
                 landed(back.at[c, pl.ds(0, count)], back_recv.at[c])
-                left(outx.at[c, pl.ds(0, count - n + 1 + deep)], far_send.at[c])
-
-    for c in range(CHUNKS):
-        left(outb.at[c, pl.ds(0, reach + half - 1)], back_send.at[c])
+            left(outx.at[:, pl.ds(0, count - n + 1 + deep)], far_send)
+
+    left(outb.at[:, pl.ds(0, reach + half - 1)], back_send)
 
 
 def fused(psi, potential, n):
@@ -593,8 +593,8 @@
             vec(CHUNKS, n), vec(CHUNKS, half - reach),
             pltpu.VMEM((n, nx, LANES), jnp.float32), pltpu.VMEM((2 * LANES, LANES), jnp.bfloat16),
             tile(CHUNKS), tile(CHUNKS),
-            dma(CHUNKS), dma(CHUNKS, 4), dma(CHUNKS), dma(CHUNKS), dma(), dma(),
-            dma(CHUNKS), dma(CHUNKS), dma(CHUNKS), dma(CHUNKS), dma(CHUNKS), dma(nx), dma(), vec(2, n),
+            dma(), dma(CHUNKS, 4), dma(), dma(CHUNKS), dma(), dma(),
+            dma(), dma(CHUNKS), dma(), dma(), dma(CHUNKS), dma(2), dma(), vec(2, n),
         ],
         compiler_params=pltpu.CompilerParams(collective_id=0, has_side_effects=True),
     )(psi.reshape(parts, nx, by * nz, orbs), potential.reshape(nx, by, nz))
@@ -610,7 +610,7 @@
 
 def fits(psi, n):
     parts, slabs, nx, by, nz, orbs = psi.shape
-    return parts == 2 and slabs == 1 and by == 2 and by * nz == LANES and orbs == LANES and orbs == n * SUB and n % GROUP == 0 and n // 2 > ITERS
+    return parts == 2 and slabs == 1 and by == 2 and by * nz == LANES and orbs == LANES and orbs == n * SUB and nx % 2 == 0 and n % GROUP == 0 and n // 2 > ITERS
 
 
 def per_device(n, psi, potential):

time: 47.8 us -> 47.6 us (level)
  no operation moved by 1% of the time
where the time goes in v6:
time: 47.6 us; the launch traced here: 47.5 us
  Pallas kernels  47.5 us (100%)
    pallas_call x1, Pallas kernels, fused(): pl.pallas_call(functools.partial(kernel, n, nx, nz), out_shape=pltpu.VMEM...  46.4 us
    pallas_call x1, Pallas kernels, fused(): pl.pallas_call(functools.partial(unpack_kernel, n, nx), out_shape=jax.Sha...  1.1 us

profile of v6, /device:TPU:0, one launch (start us, length us, event | category | flops | bytes accessed | tf_op | source)
XLA Modules:
  0.0 47.5 jit_solution(13895268698388439093)
XLA Ops:
  0.0 46.4 %shard_map.28.back = f32[2,16,8,8,128]{4,3,2,1,0:T(8,128)S(1)} custom-call(f32[2,8,128,128]{3,2,1,0:T(8,128)} %bitcast.5, f32[8,2,64]{2,1,0:T(2,128)} %bitcast.6), custom_call_target="tpu_custom_call" | custom-call | tf_op jit(solution)/shard_map/pallas_call | solution.py:585
  46.4 1.1 %shard_map.29 = f32[2,8,128,128]{3,2,1,0:T(8,128)} custom-call(f32[2,16,8,8,128]{4,3,2,1,0:T(8,128)S(1)} %shard_map.28.back), custom_call_target="tpu_custom_call" | custom-call | tf_op jit(solution)/shard_map/pallas_call | solution.py:601
